TPU v7x, 32 devices: a whole 2x2x4 slice. The times are simulated.
32 devices in a mesh: dp: 8 (over z, x), mp: 4 (over y, core).
Axes of the slice: x: 2, y: 2, z: 4, core: 2. Of those that a mesh axis runs over, the one named last changes fastest.
Arguments:
- queries: bfloat16 [16, 16, 5120], P('dp', None, 'mp')
- key_value_cache: bfloat16 [128, 2, 128, 1024], P('dp', None, None, 'mp'), may hold values from -6 to 6
- slot_tags: int32 [128], P('dp'), may hold values from 0 to 15, as said below
- span_key_value: bfloat16 [16, 2, 16, 1024], P('dp', None, None, 'mp'), may hold values from -6 to 6
- answer_id: int32 [16], P('dp'), may hold values from 0 to 127
- w_cand: bfloat16 [5120, 128], P('mp')
Outputs:
- attended: bfloat16 [16, 16, 5120], P('dp', None, 'mp')
- chain_score: float32 [16], P('dp')
- answer_tally: float32 [1, 128], P(None, 'dp')
Inputs may be any that keep to these rules, and one draw needn't show every extreme that they name: `slot_tags`: among the 16 blocks of any one index of dp, at most 2 belong to the chains o * 2 to o * 2 + 1 of any one o, and for some o every index of dp holds exactly 2 such blocks. A chain may have no cached block.
All inputs are finite; a program needn't handle non-finite values.
Results may differ from a plain program's by a relative error of at most 0.0075.
Values may be sent and summed in bfloat16 or wider, within the bound.
No kernel may reach another device: no remote copies, remote signals or barrier semaphores. Data moves between devices by JAX's collectives and lax.ppermute only.
A program may use at most 128 MiB of HBM per device.

v0:
```python
import jax
import jax.numpy as jnp
from jax import lax
from jax.sharding import PartitionSpec as P

QUERY_HEADS = 40
KEY_VALUE_HEADS = 8
HEAD_SIZE = 128
NCAND = 128
PEER = 2
SAMPLES = 16
big_neg = -1e30


def block_terms(picked, blocks, causal):
    count = picked.shape[0]
    span = picked.shape[1]
    width = blocks.shape[2]
    heads_kv = blocks.shape[3] // HEAD_SIZE
    head_group = QUERY_HEADS // KEY_VALUE_HEADS
    query_rows = picked.reshape(count, span, heads_kv, head_group, HEAD_SIZE)
    lookup_matrix = blocks[:, 0].reshape(count, width, heads_kv, HEAD_SIZE)
    value_rows = blocks[:, 1].reshape(count, width, heads_kv, HEAD_SIZE)
    logit_rows = jnp.einsum(
        "nakgd,nbkd->nkgab", query_rows, lookup_matrix, preferred_element_type=jnp.float32
    ) * HEAD_SIZE ** (-0.5)
    if causal:
        allowed = jnp.arange(span)[:, None] >= jnp.arange(width)[None, :]
        logit_rows = jnp.where(allowed, logit_rows, big_neg)
    peaks = jnp.max(logit_rows, axis=-1)
    weights = jnp.exp(logit_rows - peaks[..., None])
    totals = jnp.sum(weights, axis=-1)
    summed_scores = jnp.einsum(
        "nkgab,nbkd->nkgad",
        weights.astype(jnp.bfloat16),
        value_rows,
        preferred_element_type=jnp.float32,
    )
    return (peaks, totals, summed_scores)


def merge_items(peaks, totals, summed_scores, member):
    member_f = member.astype(jnp.float32)
    masked = jnp.where(member[:, :, None, None, None], peaks[:, None], big_neg)
    chain_peak = jnp.max(masked, axis=0)
    item_peak = jnp.einsum("nc,ckga->nkga", member_f, chain_peak, precision=lax.Precision.HIGHEST)
    present = jnp.any(member, axis=1)
    factor = jnp.where(present[:, None, None, None], jnp.exp(peaks - item_peak), 0.0)
    chain_total = jnp.einsum(
        "nc,nkga->ckga", member_f, totals * factor, precision=lax.Precision.HIGHEST
    )
    chain_sum = jnp.einsum(
        "nc,nkgad->ckgad",
        member_f,
        summed_scores * factor[..., None],
        precision=lax.Precision.HIGHEST,
    )
    return (chain_peak, chain_total, chain_sum)


def fold_pair(first, second):
    overall = jnp.maximum(first[0], second[0])
    left = jnp.exp(first[0] - overall)
    right = jnp.exp(second[0] - overall)
    total = first[1] * left + second[1] * right
    summed_scores = first[2] * left[..., None] + second[2] * right[..., None]
    return (overall, total, summed_scores)


def per_device(queries, key_value_cache, slot_tags, span_key_value, answer_id, w_cand):
    accelerator_roster = lax.axis_size("dp")
    position = lax.axis_index("dp")
    chains_here = queries.shape[0]
    features = queries.shape[2]
    slots_here = slot_tags.shape[0]
    owner_index = slot_tags // chains_here
    chain_local = slot_tags % chains_here
    owner_hot = (
        owner_index[:, None] == jnp.arange(accelerator_roster, dtype=jnp.int32)[None, :]
    ).astype(jnp.int32)
    running = jnp.cumsum(owner_hot, axis=0) - 1
    rank_in = jnp.sum(owner_hot * running, axis=1)
    target = owner_index * PEER + rank_in
    places_all = accelerator_roster * PEER
    hit = (target[:, None] == jnp.arange(places_all, dtype=jnp.int32)[None, :]).astype(jnp.int32)
    source_row = jnp.sum(hit * jnp.arange(slots_here, dtype=jnp.int32)[:, None], axis=0)
    is_filled = jnp.sum(hit, axis=0) > 0
    send_chain = jnp.where(is_filled, jnp.sum(hit * chain_local[:, None], axis=0), chains_here)
    send_blocks = key_value_cache[source_row].reshape(
        (accelerator_roster, PEER) + key_value_cache.shape[1:]
    )
    send_chain = send_chain.reshape(accelerator_roster, PEER)
    blocks = lax.all_to_all(send_blocks, "dp", split_axis=0, concat_axis=0, tiled=True)
    places = lax.all_to_all(send_chain, "dp", split_axis=0, concat_axis=0, tiled=True)
    count = places.shape[0] * places.shape[1]
    flat_places = places.reshape(count)
    picked = queries[jnp.clip(flat_places, 0, chains_here - 1)]
    peaks, totals, summed_scores = block_terms(
        picked, blocks.reshape((count,) + blocks.shape[2:]), False
    )
    lead = places.shape
    peaks, totals, summed_scores, places = (
        peaks.reshape(lead + peaks.shape[1:]),
        totals.reshape(lead + totals.shape[1:]),
        summed_scores.reshape(lead + summed_scores.shape[1:]),
        places,
    )
    count = places.shape[0] * places.shape[1]
    member = places.reshape(count)[:, None] == jnp.arange(chains_here, dtype=jnp.int32)[None, :]
    remote = merge_items(
        peaks.reshape((count,) + peaks.shape[2:]),
        totals.reshape((count,) + totals.shape[2:]),
        summed_scores.reshape((count,) + summed_scores.shape[2:]),
        member,
    )
    own_span = block_terms(queries, span_key_value, True)
    final_peak, final_total, final_sum = fold_pair(own_span, remote)
    output = final_sum / final_total[..., None]
    output = jnp.transpose(output, (0, 3, 1, 2, 4)).reshape(chains_here, queries.shape[1], features)
    attended = output.astype(jnp.bfloat16)
    span = queries.shape[1]
    partial_logits = jnp.dot(
        attended.reshape(chains_here * span, features), w_cand, preferred_element_type=jnp.float32
    )
    logit_rows = lax.psum(partial_logits, "mp").reshape(chains_here, span, NCAND)
    top_logit = jnp.max(logit_rows, axis=-1, keepdims=True)
    log_norm = top_logit[..., 0] + jnp.log(jnp.sum(jnp.exp(logit_rows - top_logit), axis=-1))
    answer_hot = (answer_id[:, None] == jnp.arange(NCAND, dtype=jnp.int32)[None, :]).astype(
        jnp.float32
    )
    chosen_logit = jnp.sum(logit_rows * answer_hot[:, None, :], axis=-1)
    chain_score = jnp.mean(chosen_logit - log_norm, axis=-1)
    prompt_count = accelerator_roster * chains_here // SAMPLES
    global_chain = position * chains_here + jnp.arange(chains_here, dtype=jnp.int32)
    prompt_hot = (
        (global_chain // SAMPLES)[:, None] == jnp.arange(prompt_count, dtype=jnp.int32)[None, :]
    ).astype(jnp.float32)
    tally_terms = jnp.dot(
        prompt_hot.T, chain_score[:, None] * answer_hot, precision=lax.Precision.HIGHEST
    )
    answer_tally = lax.psum_scatter(tally_terms, "dp", scatter_dimension=1, tiled=True)
    return (attended, chain_score, answer_tally)


def solution(mesh):
    in_specs = (
        P("dp", None, "mp"),
        P("dp", None, None, "mp"),
        P("dp"),
        P("dp", None, None, "mp"),
        P("dp"),
        P("mp", None),
    )
    out_specs = (P("dp", None, "mp"), P("dp"), P(None, "dp"))
    return jax.shard_map(
        per_device, mesh=mesh, in_specs=in_specs, out_specs=out_specs, check_vma=False
    )
```

profile of v0, /device:TPU:0, one launch (start us, length us, event | category | flops | bytes accessed | tf_op | source)
XLA Modules:
  0.0 165.2 jit_solution(9929074711548436345)
XLA Ops:
  7.2 0.0 copy-start
  7.2 0.8 and_select_fusion.1
  8.0 0.1 fusion.28
  8.1 0.2 select_reduce_fusion.3
  8.3 0.1 convert_reduce_fusion
  8.4 0.7 select_n.71
  9.1 7.3 %all-to-all-start = ((s32[8,1,2]{2,1,0:T(1,128)}), s32[8,1,2]{2,1,0:T(1,128)S(1)}, u32[]{:S(2)}, u32[]{:S(2)}) async-start(s32[8,1,2]{2,1,0:T(1,128)} %bitcast.5), calls=%async_computation | async-start | bytes 8192 | tf_op jit(solution)/shard_map/all_to_all | solution.py:94
  16.4 2.0 %gather_fusion = bf16[16,2,128,256]{3,2,1,0:T(8,128)(2,1)} fusion(bf16[16,2,128,256]{3,2,1,0:T(8,128)(2,1)S(1)} %copy-done, s32[1024]{0:T(1024)S(1)} %pad_clamp_fusion.1), kind=kCustom, calls=%fused_computation | custom fusion | bytes 4194368 | tf_op jit(solution)/shard_map/gather | solution.py:89
  18.4 3.9 %copy.89 = bf16[8,2,2,128,256]{3,4,1,2,0:T(8,128)(2,1)} copy(bf16[8,2,2,128,256]{4,3,2,1,0:T(8,128)(2,1)} %bitcast.89) | data formatting | bytes 4194304 | tf_op jit(solution)/shard_map/reshape | solution.py:89
  22.3 0.5 all-to-all-done
  22.8 5.7 %all-to-all-start.1 = ((bf16[8,2,2,128,256]{3,4,1,2,0:T(8,128)(2,1)}), bf16[8,2,2,128,256]{3,4,1,2,0:T(8,128)(2,1)}, u32[]{:S(2)}, u32[]{:S(2)}) async-start(bf16[8,2,2,128,256]{3,4,1,2,0:T(8,128)(2,1)} %copy.89), calls=%async_computation.1 | async-start | bytes 4194304 | tf_op jit(solution)/shard_map/all_to_all | solution.py:93
  28.4 0.0 reduce-scatter.4.cloned.1.call-start
  28.5 0.1 reshape.174
  28.6 0.0 copy-done.3
  28.7 0.3 fusion.64
  29.0 0.1 fusion.18
  29.0 0.1 fusion.35
  29.1 0.5 broadcast.247
  29.6 0.7 fusion.60
  30.3 0.1 min.9
  30.4 1.4 gather_fusion.1
  31.8 1.8 %reshape.177 = bf16[16,16,2,5,128]{4,3,2,1,0:T(8,128)(2,1)S(1)} reshape(bf16[16,16,1280]{2,1,0:T(8,128)(2,1)} %gather_fusion.1) | data formatting | bytes 1310720 | tf_op jit(solution)/shard_map/reshape | solution.py:21
  33.6 0.1 eq.74
  33.7 42.5 %all-to-all-done.1 = bf16[8,2,2,128,256]{3,4,1,2,0:T(8,128)(2,1)} async-done(((bf16[8,2,2,128,256]{3,4,1,2,0:T(8,128)(2,1)}), bf16[8,2,2,128,256]{3,4,1,2,0:T(8,128)(2,1)}, u32[]{:S(2)}, u32[]{:S(2)}) %all-to-all-start.1) | async-done | bytes 2097184 | tf_op jit(solution)/shard_map/all_to_all | solution.py:93
  76.2 1.7 %copy.90 = bf16[8,2,2,128,256]{3,4,1,0,2:T(8,128)(2,1)S(1)} copy(bf16[8,2,2,128,256]{3,4,1,2,0:T(8,128)(2,1)} %all-to-all-done.1) | data formatting | bytes 4194304 | tf_op jit(solution)/shard_map/all_to_all | solution.py:93
  78.0 0.2 fusion.61
  78.2 0.6 fusion.63
  78.8 0.1 select_reduce_fusion
  78.9 0.2 fusion.12
  79.2 0.8 fusion.3
  80.0 1.4 convolution_multiply_fusion
  81.5 0.0 copy-start.2
  81.5 1.3 fusion.1
  82.8 0.2 fusion.14
  83.0 0.3 fusion.10
  83.3 0.1 convert_element_type.37
  83.4 0.2 fusion.65
  83.6 10.1 %psum.7 = f32[32,128]{1,0:T(8,128)S(1)} all-reduce(f32[32,128]{1,0:T(8,128)S(1)} %fusion.65), channel_id=1, replica_groups=mesh['dp'=8,'mp'=4] {'mp'}, use_global_device_ids=true, to_apply=%region_11.12 | all-reduce | flops 4096 | bytes 32768 | tf_op jit(solution)/shard_map/psum | solution.py:125
  93.7 0.1 reduce_max.45
  93.8 0.2 exponential_reduce_fusion
  94.0 0.1 sub.76
  94.1 0.1 reduce_sum.95
  94.2 0.0 copy-start.5
  94.3 1.0 convolution_bitcast_fusion.1
  95.2 0.0 reduce-scatter.4.cloned.1.call-update
  95.2 0.7 convert_element_type.36
  96.0 61.1 %reduce-scatter.4.cloned.1.call-done = f32[16,1]{1,0:T(8,128)} async-done(((f32[128,1]{1,0:T(8,128)}), f32[16,1]{1,0:T(8,128)}) %reduce-scatter.4.cloned.1.call-update) | async-done | bytes 80
  157.1 1.3 copy.124
  (29 shorter events, 0.3 us)
Async XLA Ops:
  7.2 9.2 %copy-start = (bf16[16,2,128,256]{3,2,1,0:T(8,128)(2,1)S(1)}, bf16[16,2,128,256]{3,2,1,0:T(8,128)(2,1)}, u32[]{:S(2)}) copy-start(bf16[16,2,128,256]{3,2,1,0:T(8,128)(2,1)} %param.7) | copy-start | bytes 6291460
  9.1 13.7 %all-to-all-start = ((s32[8,1,2]{2,1,0:T(1,128)}), s32[8,1,2]{2,1,0:T(1,128)S(1)}, u32[]{:S(2)}, u32[]{:S(2)}) async-start(s32[8,1,2]{2,1,0:T(1,128)} %bitcast.5), calls=%async_computation | async-start | bytes 8192 | tf_op jit(solution)/shard_map/all_to_all | solution.py:94
  22.3 6.2 %copy-start.1 = (bf16[2,16,1280]{2,1,0:T(8,128)(2,1)S(1)}, bf16[2,16,1280]{2,1,0:T(8,128)(2,1)}, u32[]{:S(2)}) copy-start(bf16[2,16,1280]{2,1,0:T(8,128)(2,1)} %param.6) | copy-start | bytes 245764
  22.3 6.3 %copy-start.3 = (bf16[2,2,16,256]{3,2,1,0:T(8,128)(2,1)S(1)}, bf16[2,2,16,256]{3,2,1,0:T(8,128)(2,1)}, u32[]{:S(2)}) copy-start(bf16[2,2,16,256]{3,2,1,0:T(8,128)(2,1)} %param.9) | copy-start | bytes 98308
  22.3 6.8 %copy-start.4 = (s32[2]{0:T(128)S(1)}, s32[2]{0:T(128)}, u32[]{:S(2)}) copy-start(s32[2]{0:T(128)} %param.10) | copy-start | bytes 28
  22.8 53.4 %all-to-all-start.1 = ((bf16[8,2,2,128,256]{3,4,1,2,0:T(8,128)(2,1)}), bf16[8,2,2,128,256]{3,4,1,2,0:T(8,128)(2,1)}, u32[]{:S(2)}, u32[]{:S(2)}) async-start(bf16[8,2,2,128,256]{3,4,1,2,0:T(8,128)(2,1)} %copy.89), calls=%async_computation.1 | async-start | bytes 4194304 | tf_op jit(solution)/shard_map/all_to_all | solution.py:93
  28.4 128.6 %reduce-scatter.4.cloned.1.call-start = ((), (), s32[]{:S(2)}) async-start(), calls=%async_computation.3 | async-start | bytes 73728
  81.5 1.9 %copy-start.2 = (bf16[1280,128]{1,0:T(8,128)(2,1)S(1)}, bf16[1280,128]{1,0:T(8,128)(2,1)}, u32[]{:S(2)}) copy-start(bf16[1280,128]{1,0:T(8,128)(2,1)} %param.11) | copy-start | bytes 983044
  94.2 64.1 %copy-start.5 = (f32[2]{0:T(128)}, f32[2]{0:T(128)S(1)}, u32[]{:S(2)}) copy-start(f32[2]{0:T(128)S(1)} %broadcast_multiply_fusion) | copy-start | bytes 28
Sparse Core Ops, SparseCore 0:
  95.4 61.6 reduce-scatter.3
where the time goes:
time: 166 us; the launch traced here: 165 us
  waiting for transfers between devices  104 us (63%)
  local copies, waits for them, and re-layouts  14.9 us (9%)
  between operations  14.3 us (9%)
  starting transfers between devices  13 us (8%)
  blocking collectives  10.1 us (6%)
  matrix products  5.37 us (3%)
  other arithmetic  3.42 us (2%)
    unnamed x2, waiting for transfers between devices  61.1 us
    all_to_all x1, waiting for transfers between devices, per_device(): lax.all_to_all(send_blocks, 'dp', split_axis=0, concat_axis=0, tiled=True)  42.5 us
    psum x1, blocking collectives, per_device(): lax.psum(partial_logits, 'mp').reshape(chains_here, span, NCAND)  10.1 us
    all_to_all x1, starting transfers between devices, per_device(): lax.all_to_all(send_chain, 'dp', split_axis=0, concat_axis=0, tiled=True)  7.28 us
    all_to_all x1, starting transfers between devices, per_device(): lax.all_to_all(send_blocks, 'dp', split_axis=0, concat_axis=0, tiled=True)  5.66 us
    reshape x1, local copies, waits for them, and re-layouts, per_device(): key_value_cache[source_row]  3.92 us
  transfers between devices with their start and end apart: 3, of which 3 were waited for; matrix products, arithmetic and copies ran while one was open for 7% of the time, Pallas kernels for 0%

commit v1 on v0

--- a/solution.py
+++ b/solution.py
@@ -10,6 +10,12 @@
 PEER = 2
 SAMPLES = 16
 big_neg = -1e30
+
+
+def gather_and_add(array, axis):
+    blocks = lax.all_gather(array, axis, axis=0, tiled=False)
+    total = blocks.sum(axis=0)
+    return total
 
 
 def block_terms(picked, blocks, causal):
@@ -122,7 +128,7 @@
     partial_logits = jnp.dot(
         attended.reshape(chains_here * span, features), w_cand, preferred_element_type=jnp.float32
     )
-    logit_rows = lax.psum(partial_logits, "mp").reshape(chains_here, span, NCAND)
+    logit_rows = gather_and_add(partial_logits, "mp").reshape(chains_here, span, NCAND)
     top_logit = jnp.max(logit_rows, axis=-1, keepdims=True)
     log_norm = top_logit[..., 0] + jnp.log(jnp.sum(jnp.exp(logit_rows - top_logit), axis=-1))
     answer_hot = (answer_id[:, None] == jnp.arange(NCAND, dtype=jnp.int32)[None, :]).astype(

time: 166 us -> 161 us (0.970)
  blocking collectives: 10.1 us -> 5.24 us
    psum x1 -> x0, blocking collectives: 10.1 us -> none  [per_device(): lax.psum(partial_logits, 'mp').reshape(chains_here, span, NCAND)]
    all_gather x0 -> x1, blocking collectives: none -> 5.24 us  [gather_and_add(): blocks = lax.all_gather(array, axis, axis=0, tiled=False)]
where the time goes in v1:
time: 161 us; the launch traced here: 160 us
  waiting for transfers between devices  104 us (65%)
  local copies, waits for them, and re-layouts  14.9 us (9%)
  between operations  14.3 us (9%)
  starting transfers between devices  13 us (8%)
  matrix products  5.37 us (3%)
  blocking collectives  5.24 us (3%)
  other arithmetic  3.52 us (2%)
    unnamed x2, waiting for transfers between devices  61 us
    all_to_all x1, waiting for transfers between devices, per_device(): lax.all_to_all(send_blocks, 'dp', split_axis=0, concat_axis=0, tiled=True)  42.5 us
    all_to_all x1, starting transfers between devices, per_device(): lax.all_to_all(send_chain, 'dp', split_axis=0, concat_axis=0, tiled=True)  7.28 us
    all_to_all x1, starting transfers between devices, per_device(): lax.all_to_all(send_blocks, 'dp', split_axis=0, concat_axis=0, tiled=True)  5.66 us
    all_gather x1, blocking collectives, gather_and_add(): blocks = lax.all_gather(array, axis, axis=0, tiled=False)  5.24 us
    reshape x1, local copies, waits for them, and re-layouts, per_device(): key_value_cache[source_row]  3.92 us
  transfers between devices with their start and end apart: 3, of which 3 were waited for; matrix products, arithmetic and copies ran while one was open for 7% of the time, Pallas kernels for 0%

profile of v1, /device:TPU:0, one launch (start us, length us, event | category | flops | bytes accessed | tf_op | source)
XLA Modules:
  0.0 160.3 jit_solution(2322961470429245331)
XLA Ops:
  7.2 0.0 copy-start
  7.2 0.8 and_select_fusion.1
  8.0 0.1 fusion.27
  8.1 0.2 select_reduce_fusion.3
  8.3 0.1 convert_reduce_fusion
  8.4 0.7 select_n.71
  9.1 7.3 %all-to-all-start = ((s32[8,1,2]{2,1,0:T(1,128)}), s32[8,1,2]{2,1,0:T(1,128)S(1)}, u32[]{:S(2)}, u32[]{:S(2)}) async-start(s32[8,1,2]{2,1,0:T(1,128)} %bitcast.5), calls=%async_computation | async-start | bytes 8192 | tf_op jit(solution)/shard_map/all_to_all | solution.py:100
  16.4 2.0 %gather_fusion = bf16[16,2,128,256]{3,2,1,0:T(8,128)(2,1)} fusion(bf16[16,2,128,256]{3,2,1,0:T(8,128)(2,1)S(1)} %copy-done, s32[1024]{0:T(1024)S(1)} %pad_clamp_fusion.1), kind=kCustom, calls=%fused_computation | custom fusion | bytes 4194368 | tf_op jit(solution)/shard_map/gather | solution.py:95
  18.4 3.9 %copy.89 = bf16[8,2,2,128,256]{3,4,1,2,0:T(8,128)(2,1)} copy(bf16[8,2,2,128,256]{4,3,2,1,0:T(8,128)(2,1)} %bitcast.87) | data formatting | bytes 4194304 | tf_op jit(solution)/shard_map/reshape | solution.py:95
  22.3 0.5 all-to-all-done
  22.8 5.7 %all-to-all-start.1 = ((bf16[8,2,2,128,256]{3,4,1,2,0:T(8,128)(2,1)}), bf16[8,2,2,128,256]{3,4,1,2,0:T(8,128)(2,1)}, u32[]{:S(2)}, u32[]{:S(2)}) async-start(bf16[8,2,2,128,256]{3,4,1,2,0:T(8,128)(2,1)} %copy.89), calls=%async_computation.1 | async-start | bytes 4194304 | tf_op jit(solution)/shard_map/all_to_all | solution.py:99
  28.4 0.0 reduce-scatter.4.cloned.1.call-start
  28.5 0.1 reshape.181
  28.7 0.3 fusion.63
  29.0 0.1 fusion.18
  29.0 0.1 fusion.34
  29.1 0.5 broadcast.248
  29.6 0.7 fusion.59
  30.3 0.1 min.9
  30.4 1.4 gather_fusion.1
  31.8 1.8 %reshape.184 = bf16[16,16,2,5,128]{4,3,2,1,0:T(8,128)(2,1)S(1)} reshape(bf16[16,16,1280]{2,1,0:T(8,128)(2,1)} %gather_fusion.1) | data formatting | bytes 1310720 | tf_op jit(solution)/shard_map/reshape | solution.py:27
  33.6 0.1 eq.74
  33.7 42.5 %all-to-all-done.1 = bf16[8,2,2,128,256]{3,4,1,2,0:T(8,128)(2,1)} async-done(((bf16[8,2,2,128,256]{3,4,1,2,0:T(8,128)(2,1)}), bf16[8,2,2,128,256]{3,4,1,2,0:T(8,128)(2,1)}, u32[]{:S(2)}, u32[]{:S(2)}) %all-to-all-start.1) | async-done | bytes 2097184 | tf_op jit(solution)/shard_map/all_to_all | solution.py:99
  76.2 1.7 %copy.90 = bf16[8,2,2,128,256]{3,4,1,0,2:T(8,128)(2,1)S(1)} copy(bf16[8,2,2,128,256]{3,4,1,2,0:T(8,128)(2,1)} %all-to-all-done.1) | data formatting | bytes 4194304 | tf_op jit(solution)/shard_map/all_to_all | solution.py:99
  78.0 0.2 fusion.60
  78.2 0.6 fusion.62
  78.8 0.1 select_reduce_fusion
  78.9 0.2 fusion.12
  79.2 0.8 fusion.3
  80.0 1.4 convolution_multiply_fusion
  81.5 0.0 copy-start.2
  81.5 1.3 fusion.1
  82.8 0.2 fusion.14
  83.0 0.3 fusion.10
  83.3 0.1 convert_element_type.37
  83.4 0.2 fusion.64
  83.6 5.2 %all-gather = f32[128,128]{1,0:T(8,128)S(1)} all-gather(f32[32,128]{1,0:T(8,128)S(1)} %fusion.64), channel_id=2, replica_groups=mesh['dp'=8,'mp'=4] {'mp'}, dimensions={0}, use_global_device_ids=true | all-gather | bytes 81920 | tf_op jit(solution)/shard_map/all_gather | solution.py:16
  88.8 0.1 reduce_max.45
  89.0 0.2 exponential_reduce_fusion
  89.2 0.1 add.67
  89.2 0.1 multiply_reduce_fusion
  89.3 0.1 subtract_reduce_fusion
  89.5 0.0 copy-start.5
  89.5 1.0 convolution_bitcast_fusion.1
  90.4 0.0 reduce-scatter.4.cloned.1.call-update
  90.4 0.7 convert_element_type.36
  91.2 60.9 %reduce-scatter.4.cloned.1.call-done = f32[16,1]{1,0:T(8,128)} async-done(((f32[128,1]{1,0:T(8,128)}), f32[16,1]{1,0:T(8,128)}) %reduce-scatter.4.cloned.1.call-update) | async-done | bytes 80
  152.1 1.3 copy.124
  (31 shorter events, 0.3 us)
Async XLA Ops:
  7.2 9.2 %copy-start = (bf16[16,2,128,256]{3,2,1,0:T(8,128)(2,1)S(1)}, bf16[16,2,128,256]{3,2,1,0:T(8,128)(2,1)}, u32[]{:S(2)}) copy-start(bf16[16,2,128,256]{3,2,1,0:T(8,128)(2,1)} %param.7) | copy-start | bytes 6291460
  9.1 13.7 %all-to-all-start = ((s32[8,1,2]{2,1,0:T(1,128)}), s32[8,1,2]{2,1,0:T(1,128)S(1)}, u32[]{:S(2)}, u32[]{:S(2)}) async-start(s32[8,1,2]{2,1,0:T(1,128)} %bitcast.5), calls=%async_computation | async-start | bytes 8192 | tf_op jit(solution)/shard_map/all_to_all | solution.py:100
  22.3 6.2 %copy-start.1 = (bf16[2,16,1280]{2,1,0:T(8,128)(2,1)S(1)}, bf16[2,16,1280]{2,1,0:T(8,128)(2,1)}, u32[]{:S(2)}) copy-start(bf16[2,16,1280]{2,1,0:T(8,128)(2,1)} %param.6) | copy-start | bytes 245764
  22.3 6.3 %copy-start.3 = (bf16[2,2,16,256]{3,2,1,0:T(8,128)(2,1)S(1)}, bf16[2,2,16,256]{3,2,1,0:T(8,128)(2,1)}, u32[]{:S(2)}) copy-start(bf16[2,2,16,256]{3,2,1,0:T(8,128)(2,1)} %param.9) | copy-start | bytes 98308
  22.3 6.8 %copy-start.4 = (s32[2]{0:T(128)S(1)}, s32[2]{0:T(128)}, u32[]{:S(2)}) copy-start(s32[2]{0:T(128)} %param.10) | copy-start | bytes 28
  22.8 53.4 %all-to-all-start.1 = ((bf16[8,2,2,128,256]{3,4,1,2,0:T(8,128)(2,1)}), bf16[8,2,2,128,256]{3,4,1,2,0:T(8,128)(2,1)}, u32[]{:S(2)}, u32[]{:S(2)}) async-start(bf16[8,2,2,128,256]{3,4,1,2,0:T(8,128)(2,1)} %copy.89), calls=%async_computation.1 | async-start | bytes 4194304 | tf_op jit(solution)/shard_map/all_to_all | solution.py:99
  28.4 123.7 %reduce-scatter.4.cloned.1.call-start = ((), (), s32[]{:S(2)}) async-start(), calls=%async_computation.3 | async-start | bytes 73728
  81.5 1.9 %copy-start.2 = (bf16[1280,128]{1,0:T(8,128)(2,1)S(1)}, bf16[1280,128]{1,0:T(8,128)(2,1)}, u32[]{:S(2)}) copy-start(bf16[1280,128]{1,0:T(8,128)(2,1)} %param.11) | copy-start | bytes 983044
  89.5 63.9 %copy-start.5 = (f32[2]{0:T(128)}, f32[2]{0:T(128)S(1)}, u32[]{:S(2)}) copy-start(f32[2]{0:T(128)S(1)} %broadcast_multiply_fusion) | copy-start | bytes 28
Sparse Core Ops, SparseCore 0:
  90.6 61.5 reduce-scatter.3
